TPU v7x, 32 devices: a whole 2x2x4 slice. The times are simulated.
32 devices in a mesh: rows: 8 (over z, y), grp: 4 (over x, core).
Axes of the slice: x: 2, y: 2, z: 4, core: 2. Of those that a mesh axis runs over, the one named last changes fastest.
Arguments:
- basis: float32 [32, 65536], P(None, ('rows', 'grp')), may hold values from -0.03125 to 0.03125, as said below
- core: float32 [32, 32], replicated, may hold values from -0.3 to 4
- snapshots: bfloat16 [4, 32, 65536], P(None, 'grp', 'rows'), may hold values from -16 to 16
Outputs:
- new_basis: float32 [32, 65536], P(None, ('rows', 'grp'))
- new_core: float32 [32, 32], replicated
- first_coeffs: float32 [4, 32, 32], replicated
Inputs may be any that keep to these rules, and one draw needn't show every extreme that they name: `basis`: rows orthonormal up to float32 rounding.
All inputs are finite; a program needn't handle non-finite values.
Results may differ from a plain program's by a relative error of at most 0.0003.
Values may be sent and summed in bfloat16 or wider, within the bound.
A program may use at most 64 MiB of HBM per device.

v0:
```python
import jax
import jax.numpy as jnp
from jax import lax
from jax.sharding import PartitionSpec as P

BATCHES = 4
epsilon = 1e-06


def contract_rows(left, right):
    return lax.dot_general(
        left,
        right,
        (((1,), (1,)), ((), ())),
        precision=lax.Precision.HIGHEST,
        preferred_element_type=jnp.float32,
    )


def matmul(left, right):
    return jnp.dot(left, right, precision=lax.Precision.HIGHEST, preferred_element_type=jnp.float32)


def lower_solve(factor, right):
    return lax.linalg.triangular_solve(factor, right, left_side=True, lower=True)


def small_update(core_now, total, lower):
    rank = core_now.shape[0]
    cols = lower.shape[0]
    top = jnp.concatenate([core_now, total], axis=1)
    bottom = jnp.concatenate([jnp.zeros((cols, rank), jnp.float32), lower.T], axis=1)
    stacked = jnp.concatenate([top, bottom], axis=0)
    moment = matmul(stacked, stacked.T)
    leading = moment[:, :rank]
    factor = jnp.linalg.cholesky(matmul(leading.T, leading))
    rotation = lower_solve(factor, leading.T).T
    fresh_core = jnp.linalg.cholesky(matmul(rotation.T, matmul(moment, rotation)))
    return (rotation, fresh_core)


def body(basis, core, snapshots):
    rank = basis.shape[0]
    basis_now = basis
    core_now = core
    firsts = []
    gram_basis = lax.psum(contract_rows(basis_now, basis_now), ("rows", "grp"))
    for batch in range(BATCHES):
        columns = lax.all_to_all(snapshots[batch], "grp", split_axis=1, concat_axis=0, tiled=True)
        raw = columns.astype(jnp.float32)
        raw_cross, raw_gram = lax.psum(
            (contract_rows(basis_now, raw), contract_rows(raw, raw)), ("rows", "grp")
        )
        inverse = lax.rsqrt(jnp.diagonal(raw_gram) + epsilon)
        scaled = raw * inverse[:, None]
        cross = raw_cross * inverse[None, :]
        gram_raw = raw_gram * inverse[:, None] * inverse[None, :]
        second = cross - matmul(gram_basis, cross)
        total = cross + second
        basis_cross = cross - matmul(gram_basis, total)
        gram = (
            gram_raw
            - matmul(total.T, cross)
            - matmul(cross.T, total)
            + matmul(total.T, matmul(gram_basis, total))
        )
        twice = scaled - matmul(total.T, basis_now)
        lower = jnp.linalg.cholesky(gram)
        fresh = lower_solve(lower, twice)
        rotation, core_now = small_update(core_now, total, lower)
        cross_fresh = lower_solve(lower, basis_cross.T).T
        halfway = lower_solve(lower, gram)
        gram_fresh = lower_solve(lower, halfway.T).T
        upper_block = jnp.concatenate([gram_basis, cross_fresh], axis=1)
        lower_block = jnp.concatenate([cross_fresh.T, gram_fresh], axis=1)
        combined = jnp.concatenate([upper_block, lower_block], axis=0)
        gram_basis = matmul(rotation.T, matmul(combined, rotation))
        firsts.append(cross)
        basis_now = matmul(rotation[:rank].T, basis_now) + matmul(rotation[rank:].T, fresh)
    return (basis_now, core_now, jnp.stack(firsts, axis=0))


def solution(mesh):
    return jax.shard_map(
        body,
        mesh=mesh,
        in_specs=(P(None, ("rows", "grp")), P(), P(None, "grp", "rows")),
        out_specs=(P(None, ("rows", "grp")), P(), P()),
        check_vma=False,
    )
```

profile of v0, /device:TPU:0, one launch (start us, length us, event | category | flops | bytes accessed | tf_op | source)
XLA Modules:
  0.0 283.6 jit_solution(1562950860485663812)
XLA Ops:
  0.6 1.9 fusion.229
  2.6 4.4 %all-to-all-start = ((bf16[8,4,2048]{2,0,1:T(8,128)(2,1)}), bf16[8,4,2048]{2,0,1:T(8,128)(2,1)S(1)}, u32[]{:S(2)}, u32[]{:S(2)}) async-start(bf16[8,4,2048]{2,0,1:T(8,128)(2,1)} %bitcast), calls=%async_computation | async-start | bytes 262144 | tf_op jit(solution)/shard_map/all_to_all | solution.py:49
  7.4 4.1 %all-to-all-done = bf16[8,4,2048]{2,0,1:T(8,128)(2,1)S(1)} async-done(((bf16[8,4,2048]{2,0,1:T(8,128)(2,1)}), bf16[8,4,2048]{2,0,1:T(8,128)(2,1)S(1)}, u32[]{:S(2)}, u32[]{:S(2)}) %all-to-all-start) | async-done | bytes 131104 | tf_op jit(solution)/shard_map/all_to_all | solution.py:49
  11.6 3.3 %all-to-all-start.1 = ((bf16[8,4,2048]{2,0,1:T(8,128)(2,1)}), bf16[8,4,2048]{2,0,1:T(8,128)(2,1)S(1)}, u32[]{:S(2)}, u32[]{:S(2)}) async-start(bf16[8,4,2048]{2,0,1:T(8,128)(2,1)} %bitcast.15), calls=%async_computation.1 | async-start | bytes 262144 | tf_op jit(solution)/shard_map/all_to_all | solution.py:49
  15.3 42.1 %all-reduce.7 = (f32[32,32]{1,0:T(8,128)S(1)}, f32[32,32]{0,1:T(8,128)S(1)}, f32[32,32]{0,1:T(8,128)S(1)}) all-reduce(f32[32,32]{1,0:T(8,128)S(1)} %fusion.230, f32[32,32]{0,1:T(8,128)S(1)} %fusion.18, f32[32,32]{0,1:T(8,128)S(1)} %fusion.16), channel_id=1, replica_groups=mesh['rows'=8,'grp'=4] {'rows','grp'}, use_global_device_ids=true, to_apply=%region_2.0 | all-reduce | flops 3072 | bytes 24576 | tf_op jit(solution)/shard_map/psum | solution.py:47
  59.3 2.9 %cholesky.194 = f32[32,32]{1,0:T(8,128)S(1)} custom-call(f32[32,32]{1,0:T(8,128)S(1)} %fusion.134), custom_call_target="Cholesky" | custom-call | tf_op jit(solution)/shard_map/jit(cholesky)/cholesky | solution.py:68
  63.6 2.4 custom-call.34
  67.2 2.9 %cholesky.205 = f32[32,32]{1,0:T(8,128)S(1)} custom-call(f32[32,32]{1,0:T(8,128)S(1)} %fusion.133), custom_call_target="Cholesky" | custom-call | tf_op jit(solution)/shard_map/jit(cholesky)/cholesky | solution.py:36
  71.4 2.4 custom-call.33
  76.5 3.5 %all-to-all-start.2 = ((bf16[8,4,2048]{2,0,1:T(8,128)(2,1)}), bf16[8,4,2048]{2,0,1:T(8,128)(2,1)S(1)}, u32[]{:S(2)}, u32[]{:S(2)}) async-start(bf16[8,4,2048]{2,0,1:T(8,128)(2,1)} %bitcast.39), calls=%async_computation.2 | async-start | bytes 262144 | tf_op jit(solution)/shard_map/all_to_all | solution.py:49
  80.4 41.5 %all-reduce.6 = (f32[32,32]{0,1:T(8,128)S(1)}, f32[32,32]{0,1:T(8,128)S(1)}) all-reduce(f32[32,32]{0,1:T(8,128)S(1)} %fusion.14, f32[32,32]{0,1:T(8,128)S(1)} %fusion.12), channel_id=1, replica_groups=mesh['rows'=8,'grp'=4] {'rows','grp'}, use_global_device_ids=true, to_apply=%region_5.9 | all-reduce | flops 2048 | bytes 16384 | tf_op jit(solution)/shard_map/psum | solution.py:51
  123.5 2.9 %cholesky.216 = f32[32,32]{1,0:T(8,128)S(1)} custom-call(f32[32,32]{1,0:T(8,128)S(1)} %fusion.129), custom_call_target="Cholesky" | custom-call | tf_op jit(solution)/shard_map/jit(cholesky)/cholesky | solution.py:38
  128.5 2.9 %cholesky.227 = f32[32,32]{1,0:T(8,128)S(1)} custom-call(f32[32,32]{1,0:T(8,128)S(1)} %fusion.121), custom_call_target="Cholesky" | custom-call | tf_op jit(solution)/shard_map/jit(cholesky)/cholesky | solution.py:68
  132.8 2.4 custom-call.39
  136.4 2.9 %cholesky.238 = f32[32,32]{1,0:T(8,128)S(1)} custom-call(f32[32,32]{1,0:T(8,128)S(1)} %fusion.120), custom_call_target="Cholesky" | custom-call | tf_op jit(solution)/shard_map/jit(cholesky)/cholesky | solution.py:36
  140.7 2.4 custom-call.38
  145.7 3.5 %all-to-all-start.3 = ((bf16[8,4,2048]{2,0,1:T(8,128)(2,1)}), bf16[8,4,2048]{2,0,1:T(8,128)(2,1)S(1)}, u32[]{:S(2)}, u32[]{:S(2)}) async-start(bf16[8,4,2048]{2,0,1:T(8,128)(2,1)} %bitcast.63), calls=%async_computation.3 | async-start | bytes 262144 | tf_op jit(solution)/shard_map/all_to_all | solution.py:49
  149.7 40.7 %all-reduce.5 = (f32[32,32]{0,1:T(8,128)S(1)}, f32[32,32]{0,1:T(8,128)S(1)}) all-reduce(f32[32,32]{0,1:T(8,128)S(1)} %fusion.10, f32[32,32]{0,1:T(8,128)S(1)} %fusion.8), channel_id=1, replica_groups=mesh['rows'=8,'grp'=4] {'rows','grp'}, use_global_device_ids=true, to_apply=%region_7.12 | all-reduce | flops 2048 | bytes 16384 | tf_op jit(solution)/shard_map/psum | solution.py:51
  192.0 2.9 %cholesky.249 = f32[32,32]{1,0:T(8,128)S(1)} custom-call(f32[32,32]{1,0:T(8,128)S(1)} %fusion.116), custom_call_target="Cholesky" | custom-call | tf_op jit(solution)/shard_map/jit(cholesky)/cholesky | solution.py:38
  197.0 2.9 %cholesky.260 = f32[32,32]{1,0:T(8,128)S(1)} custom-call(f32[32,32]{1,0:T(8,128)S(1)} %fusion.108), custom_call_target="Cholesky" | custom-call | tf_op jit(solution)/shard_map/jit(cholesky)/cholesky | solution.py:68
  201.2 2.4 custom-call.44
  204.8 2.9 %cholesky.271 = f32[32,32]{1,0:T(8,128)S(1)} custom-call(f32[32,32]{1,0:T(8,128)S(1)} %fusion.107), custom_call_target="Cholesky" | custom-call | tf_op jit(solution)/shard_map/jit(cholesky)/cholesky | solution.py:36
  209.1 2.4 custom-call.43
  214.6 39.8 %all-reduce.4 = (f32[32,32]{0,1:T(8,128)S(1)}, f32[32,32]{0,1:T(8,128)S(1)}) all-reduce(f32[32,32]{0,1:T(8,128)S(1)} %fusion.6, f32[32,32]{0,1:T(8,128)S(1)} %fusion.4), channel_id=1, replica_groups=mesh['rows'=8,'grp'=4] {'rows','grp'}, use_global_device_ids=true, to_apply=%region_9.14 | all-reduce | flops 2048 | bytes 16384 | tf_op jit(solution)/shard_map/psum | solution.py:51
  256.1 2.9 %cholesky.282 = f32[32,32]{1,0:T(8,128)S(1)} custom-call(f32[32,32]{1,0:T(8,128)S(1)} %fusion.103), custom_call_target="Cholesky" | custom-call | tf_op jit(solution)/shard_map/jit(cholesky)/cholesky | solution.py:38
  261.8 2.9 %cholesky.293 = f32[32,32]{1,0:T(8,128)S(1)} custom-call(f32[32,32]{1,0:T(8,128)S(1)} %fusion.95), custom_call_target="Cholesky" | custom-call | tf_op jit(solution)/shard_map/jit(cholesky)/cholesky | solution.py:68
  266.0 2.4 custom-call.49
  269.0 2.9 %cholesky.304 = f32[32,32]{1,0:T(8,128)S(1)} custom-call(f32[32,32]{1,0:T(8,128)S(1)} %fusion.94), custom_call_target="Cholesky" | custom-call | tf_op jit(solution)/shard_map/jit(cholesky)/cholesky | solution.py:36
  273.3 2.4 custom-call.48
  276.5 2.9 %cholesky.315 = f32[32,32]{1,0:T(8,128)S(1)} custom-call(f32[32,32]{1,0:T(8,128)S(1)} %fusion.88), custom_call_target="Cholesky" | custom-call | tf_op jit(solution)/shard_map/jit(cholesky)/cholesky | solution.py:38
  280.1 1.3 select_select_fusion.4
  282.5 1.1 convolution_add_fusion
  (170 shorter events, 40.3 us)
Async XLA Ops:
  0.6 6.4 %copy-start = (f32[32,2048]{1,0:T(8,128)S(1)}, f32[32,2048]{1,0:T(8,128)}, u32[]{:S(2)}) copy-start(f32[32,2048]{1,0:T(8,128)} %param.10) | copy-start | bytes 786436
  2.6 4.4 %copy-start.1 = (f32[32,32]{1,0:T(8,128)S(1)}, f32[32,32]{1,0:T(8,128)}, u32[]{:S(2)}) copy-start(f32[32,32]{1,0:T(8,128)} %param.11) | copy-start | bytes 12292
  2.6 9.0 %all-to-all-start = ((bf16[8,4,2048]{2,0,1:T(8,128)(2,1)}), bf16[8,4,2048]{2,0,1:T(8,128)(2,1)S(1)}, u32[]{:S(2)}, u32[]{:S(2)}) async-start(bf16[8,4,2048]{2,0,1:T(8,128)(2,1)} %bitcast), calls=%async_computation | async-start | bytes 262144 | tf_op jit(solution)/shard_map/all_to_all | solution.py:49
  11.6 64.9 %all-to-all-start.1 = ((bf16[8,4,2048]{2,0,1:T(8,128)(2,1)}), bf16[8,4,2048]{2,0,1:T(8,128)(2,1)S(1)}, u32[]{:S(2)}, u32[]{:S(2)}) async-start(bf16[8,4,2048]{2,0,1:T(8,128)(2,1)} %bitcast.15), calls=%async_computation.1 | async-start | bytes 262144 | tf_op jit(solution)/shard_map/all_to_all | solution.py:49
  76.5 69.2 %all-to-all-start.2 = ((bf16[8,4,2048]{2,0,1:T(8,128)(2,1)}), bf16[8,4,2048]{2,0,1:T(8,128)(2,1)S(1)}, u32[]{:S(2)}, u32[]{:S(2)}) async-start(bf16[8,4,2048]{2,0,1:T(8,128)(2,1)} %bitcast.39), calls=%async_computation.2 | async-start | bytes 262144 | tf_op jit(solution)/shard_map/all_to_all | solution.py:49
  145.7 68.5 %all-to-all-start.3 = ((bf16[8,4,2048]{2,0,1:T(8,128)(2,1)}), bf16[8,4,2048]{2,0,1:T(8,128)(2,1)S(1)}, u32[]{:S(2)}, u32[]{:S(2)}) async-start(bf16[8,4,2048]{2,0,1:T(8,128)(2,1)} %bitcast.63), calls=%async_computation.3 | async-start | bytes 262144 | tf_op jit(solution)/shard_map/all_to_all | solution.py:49
where the time goes:
time: 285 us; the launch traced here: 284 us
  blocking collectives  164 us (58%)
  other arithmetic  71.8 us (25%)
  matrix products  20.3 us (7%)
  starting transfers between devices  14.7 us (5%)
  local copies, waits for them, and re-layouts  7.12 us (2%)
  waiting for transfers between devices  4.15 us (1%)
    psum x3, blocking collectives, body(): lax.psum((contract_rows(basis_now, raw), contract_rows(raw, raw)), ('rows...  122 us
    psum x1, blocking collectives, body(): gram_basis = lax.psum(contract_rows(basis_now, basis_now), ('rows', 'grp'))  42.1 us
    another operation x16, other arithmetic, lower_solve(): lax.linalg.triangular_solve(factor, right, left_side=True, lower=True)  24.7 us
    all_to_all x4, starting transfers between devices, body(): lax.all_to_all(snapshots[batch], 'grp', split_axis=1, concat_axis=0, tile...  14.7 us
    another operation x12, other arithmetic, small_update(): jnp.linalg.cholesky(matmul(rotation.T, matmul(moment, rotation)))  14.7 us
    another operation x12, other arithmetic, small_update(): factor = jnp.linalg.cholesky(matmul(leading.T, leading))  14.4 us
    another operation x12, other arithmetic, body(): lower = jnp.linalg.cholesky(gram)  14.4 us
    dot_general x54, matrix products, matmul(): jnp.dot(left, right, precision=lax.Precision.HIGHEST, preferred_element_t...  13.7 us
  transfers between devices with their start and end apart: 4, of which 1 were waited for; matrix products, arithmetic and copies ran while one was open for 24% of the time, Pallas kernels for 0%

commit v1 on v0

--- a/solution.py
+++ b/solution.py
@@ -49,7 +49,7 @@
         columns = lax.all_to_all(snapshots[batch], "grp", split_axis=1, concat_axis=0, tiled=True)
         raw = columns.astype(jnp.float32)
         raw_cross, raw_gram = lax.psum(
-            (contract_rows(basis_now, raw), contract_rows(raw, raw)), ("rows", "grp")
+            lax.psum((contract_rows(basis_now, raw), contract_rows(raw, raw)), "grp"), "rows"
         )
         inverse = lax.rsqrt(jnp.diagonal(raw_gram) + epsilon)
         scaled = raw * inverse[:, None]

time: 285 us -> 340 us (1.19)
  blocking collectives: 164 us -> 224 us
  waiting for transfers between devices: 4.15 us -> 0.01 us
    psum x3 -> x8, blocking collectives: 122 us -> 182 us  [the longest x4 136 us: body(): lax.psum(lax.psum((contract_rows(basis_now, raw), contract_rows(raw, raw)...]
    all_to_all x4, waiting for transfers between devices: 4.15 us -> 0.01 us  [body(): lax.all_to_all(snapshots[batch], 'grp', split_axis=1, concat_axis=0, tile...]
  transfers between devices with their start and end apart: 4 -> 4, of which waited for: 1 -> 0; matrix products, arithmetic and copies ran while one was open for 24% -> 20% of each run, Pallas kernels for 0% -> 0%
where the time goes in v1:
time: 340 us; the launch traced here: 339 us
  blocking collectives  224 us (66%)
  other arithmetic  71.8 us (21%)
  matrix products  20.2 us (6%)
  starting transfers between devices  14.6 us (4%)
  local copies, waits for them, and re-layouts  7.11 us (2%)
    psum x4, blocking collectives, body(): lax.psum(lax.psum((contract_rows(basis_now, raw), contract_rows(raw, raw)...  136 us
    psum x4, blocking collectives, body(): lax.psum((contract_rows(basis_now, raw), contract_rows(raw, raw)), 'grp')  46 us
    psum x1, blocking collectives, body(): gram_basis = lax.psum(contract_rows(basis_now, basis_now), ('rows', 'grp'))  41.7 us
    another operation x16, other arithmetic, lower_solve(): lax.linalg.triangular_solve(factor, right, left_side=True, lower=True)  24.7 us
    another operation x12, other arithmetic, small_update(): jnp.linalg.cholesky(matmul(rotation.T, matmul(moment, rotation)))  14.7 us
    all_to_all x4, starting transfers between devices, body(): lax.all_to_all(snapshots[batch], 'grp', split_axis=1, concat_axis=0, tile...  14.6 us
    another operation x12, other arithmetic, small_update(): factor = jnp.linalg.cholesky(matmul(leading.T, leading))  14.4 us
    another operation x12, other arithmetic, body(): lower = jnp.linalg.cholesky(gram)  14.4 us
  transfers between devices with their start and end apart: 4, of which 0 were waited for; matrix products, arithmetic and copies ran while one was open for 20% of the time, Pallas kernels for 0%

profile of v1, /device:TPU:0, one launch (start us, length us, event | category | flops | bytes accessed | tf_op | source)
XLA Modules:
  0.0 338.7 jit_solution(9093868644817619418)
XLA Ops:
  2.6 4.4 %all-to-all-start = ((bf16[8,4,2048]{2,0,1:T(8,128)(2,1)}), bf16[8,4,2048]{2,0,1:T(8,128)(2,1)S(1)}, u32[]{:S(2)}, u32[]{:S(2)}) async-start(bf16[8,4,2048]{2,0,1:T(8,128)(2,1)} %bitcast), calls=%async_computation | async-start | bytes 262144 | tf_op jit(solution)/shard_map/all_to_all | solution.py:49
  7.4 41.7 %psum.123 = f32[32,32]{1,0:T(8,128)S(1)} all-reduce(f32[32,32]{1,0:T(8,128)S(1)} %fusion.230), channel_id=1, replica_groups=mesh['rows'=8,'grp'=4] {'rows','grp'}, use_global_device_ids=true, to_apply=%region_4.0 | all-reduce | flops 1024 | bytes 8192 | tf_op jit(solution)/shard_map/psum | solution.py:47
  49.1 3.6 %all-to-all-start.1 = ((bf16[8,4,2048]{2,0,1:T(8,128)(2,1)}), bf16[8,4,2048]{2,0,1:T(8,128)(2,1)S(1)}, u32[]{:S(2)}, u32[]{:S(2)}) async-start(bf16[8,4,2048]{2,0,1:T(8,128)(2,1)} %bitcast.15), calls=%async_computation.1 | async-start | bytes 262144 | tf_op jit(solution)/shard_map/all_to_all | solution.py:49
  53.1 11.9 %all-reduce.11 = (f32[32,32]{0,1:T(8,128)S(1)}, f32[32,32]{0,1:T(8,128)S(1)}) all-reduce(f32[32,32]{0,1:T(8,128)S(1)} %fusion.18, f32[32,32]{0,1:T(8,128)S(1)} %fusion.16), channel_id=1, replica_groups=mesh['rows'=8,'grp'=4] {'grp'}, use_global_device_ids=true, to_apply=%region_0.0 | all-reduce | flops 2048 | bytes 16384 | tf_op jit(solution)/shard_map/psum | solution.py:52
  65.0 36.5 %all-reduce.7 = (f32[32,32]{0,1:T(8,128)S(1)}, f32[32,32]{0,1:T(8,128)S(1)}) all-reduce(f32[32,32]{0,1:T(8,128)S(1)} %get-tuple-element.27, f32[32,32]{0,1:T(8,128)S(1)} %get-tuple-element.28), channel_id=1, replica_groups=mesh['rows'=8,'grp'=4] {'rows'}, use_global_device_ids=true, to_apply=%region_1.0 | all-reduce | flops 2048 | bytes 16384 | tf_op jit(solution)/shard_map/psum | solution.py:51
  103.5 2.9 cholesky.194
  107.7 2.4 custom-call.34
  111.3 2.9 cholesky.205
  115.6 2.4 custom-call.33
  120.6 3.3 all-to-all-start.2
  124.4 11.9 %all-reduce.10 = (f32[32,32]{0,1:T(8,128)S(1)}, f32[32,32]{0,1:T(8,128)S(1)}) all-reduce(f32[32,32]{0,1:T(8,128)S(1)} %fusion.14, f32[32,32]{0,1:T(8,128)S(1)} %fusion.12), channel_id=1, replica_groups=mesh['rows'=8,'grp'=4] {'grp'}, use_global_device_ids=true, to_apply=%region_7.11 | all-reduce | flops 2048 | bytes 16384 | tf_op jit(solution)/shard_map/psum | solution.py:52
  136.3 33.1 %all-reduce.6 = (f32[32,32]{0,1:T(8,128)S(1)}, f32[32,32]{0,1:T(8,128)S(1)}) all-reduce(f32[32,32]{0,1:T(8,128)S(1)} %get-tuple-element.25, f32[32,32]{0,1:T(8,128)S(1)} %get-tuple-element.26), channel_id=1, replica_groups=mesh['rows'=8,'grp'=4] {'rows'}, use_global_device_ids=true, to_apply=%region_8.12 | all-reduce | flops 2048 | bytes 16384 | tf_op jit(solution)/shard_map/psum | solution.py:51
  170.9 2.9 cholesky.216
  175.9 2.9 cholesky.227
  180.2 2.4 custom-call.39
  183.8 2.9 cholesky.238
  188.1 2.4 custom-call.38
  193.1 3.3 all-to-all-start.3
  196.9 11.9 %all-reduce.9 = (f32[32,32]{0,1:T(8,128)S(1)}, f32[32,32]{0,1:T(8,128)S(1)}) all-reduce(f32[32,32]{0,1:T(8,128)S(1)} %fusion.10, f32[32,32]{0,1:T(8,128)S(1)} %fusion.8), channel_id=1, replica_groups=mesh['rows'=8,'grp'=4] {'grp'}, use_global_device_ids=true, to_apply=%region_11.16 | all-reduce | flops 2048 | bytes 16384 | tf_op jit(solution)/shard_map/psum | solution.py:52
  208.8 33.2 %all-reduce.5 = (f32[32,32]{0,1:T(8,128)S(1)}, f32[32,32]{0,1:T(8,128)S(1)}) all-reduce(f32[32,32]{0,1:T(8,128)S(1)} %get-tuple-element.23, f32[32,32]{0,1:T(8,128)S(1)} %get-tuple-element.24), channel_id=1, replica_groups=mesh['rows'=8,'grp'=4] {'rows'}, use_global_device_ids=true, to_apply=%region_12.17 | all-reduce | flops 2048 | bytes 16384 | tf_op jit(solution)/shard_map/psum | solution.py:51
  243.6 2.9 cholesky.249
  248.6 2.9 cholesky.260
  252.9 2.4 custom-call.44
  256.5 2.9 cholesky.271
  260.7 2.4 custom-call.43
  266.2 10.3 %all-reduce.8 = (f32[32,32]{0,1:T(8,128)S(1)}, f32[32,32]{0,1:T(8,128)S(1)}) all-reduce(f32[32,32]{0,1:T(8,128)S(1)} %fusion.6, f32[32,32]{0,1:T(8,128)S(1)} %fusion.4), channel_id=1, replica_groups=mesh['rows'=8,'grp'=4] {'grp'}, use_global_device_ids=true, to_apply=%region_15.20 | all-reduce | flops 2048 | bytes 16384 | tf_op jit(solution)/shard_map/psum | solution.py:52
  276.5 33.1 %all-reduce.4 = (f32[32,32]{0,1:T(8,128)S(1)}, f32[32,32]{0,1:T(8,128)S(1)}) all-reduce(f32[32,32]{0,1:T(8,128)S(1)} %get-tuple-element.21, f32[32,32]{0,1:T(8,128)S(1)} %get-tuple-element.22), channel_id=1, replica_groups=mesh['rows'=8,'grp'=4] {'rows'}, use_global_device_ids=true, to_apply=%region_16.21 | all-reduce | flops 2048 | bytes 16384 | tf_op jit(solution)/shard_map/psum | solution.py:51
  311.2 2.9 cholesky.282
  316.9 2.9 cholesky.293
  321.1 2.4 custom-call.49
  324.2 2.9 cholesky.304
  331.6 2.9 cholesky.315
  (175 shorter events, 47.0 us)
Async XLA Ops:
  0.6 6.4 %copy-start = (f32[32,2048]{1,0:T(8,128)S(1)}, f32[32,2048]{1,0:T(8,128)}, u32[]{:S(2)}) copy-start(f32[32,2048]{1,0:T(8,128)} %param.10) | copy-start | bytes 786436
  2.6 4.4 %copy-start.1 = (f32[32,32]{1,0:T(8,128)S(1)}, f32[32,32]{1,0:T(8,128)}, u32[]{:S(2)}) copy-start(f32[32,32]{1,0:T(8,128)} %param.11) | copy-start | bytes 12292
  2.6 46.5 %all-to-all-start = ((bf16[8,4,2048]{2,0,1:T(8,128)(2,1)}), bf16[8,4,2048]{2,0,1:T(8,128)(2,1)S(1)}, u32[]{:S(2)}, u32[]{:S(2)}) async-start(bf16[8,4,2048]{2,0,1:T(8,128)(2,1)} %bitcast), calls=%async_computation | async-start | bytes 262144 | tf_op jit(solution)/shard_map/all_to_all | solution.py:49
  49.1 71.6 %all-to-all-start.1 = ((bf16[8,4,2048]{2,0,1:T(8,128)(2,1)}), bf16[8,4,2048]{2,0,1:T(8,128)(2,1)S(1)}, u32[]{:S(2)}, u32[]{:S(2)}) async-start(bf16[8,4,2048]{2,0,1:T(8,128)(2,1)} %bitcast.15), calls=%async_computation.1 | async-start | bytes 262144 | tf_op jit(solution)/shard_map/all_to_all | solution.py:49
  120.6 72.5 %all-to-all-start.2 = ((bf16[8,4,2048]{2,0,1:T(8,128)(2,1)}), bf16[8,4,2048]{2,0,1:T(8,128)(2,1)S(1)}, u32[]{:S(2)}, u32[]{:S(2)}) async-start(bf16[8,4,2048]{2,0,1:T(8,128)(2,1)} %bitcast.39), calls=%async_computation.2 | async-start | bytes 262144 | tf_op jit(solution)/shard_map/all_to_all | solution.py:49
  193.1 72.7 %all-to-all-start.3 = ((bf16[8,4,2048]{2,0,1:T(8,128)(2,1)}), bf16[8,4,2048]{2,0,1:T(8,128)(2,1)S(1)}, u32[]{:S(2)}, u32[]{:S(2)}) async-start(bf16[8,4,2048]{2,0,1:T(8,128)(2,1)} %bitcast.63), calls=%async_computation.3 | async-start | bytes 262144 | tf_op jit(solution)/shard_map/all_to_all | solution.py:49
